TPU v7x, 32 devices: a whole 2x2x4 slice. The times are simulated.
32 devices in a mesh: rep: 2 (over core), seq: 16 (over z, y, x).
Axes of the slice: x: 2, y: 2, z: 4, core: 2. Of those that a mesh axis runs over, the one named last changes fastest.
Arguments:
- queries: bfloat16 [4096, 8192], P(('rep', 'seq')), parts along dimension 0, may hold values from -180 to 180
- keys: bfloat16 [16384, 1024], P(('rep', 'seq')), parts along dimension 0, may hold values from -6 to 6
- values: bfloat16 [16384, 1024], P(('rep', 'seq')), parts along dimension 0, may hold values from -6 to 6
- vertical: int32 [128, 64], P('rep'), parts along dimension 0, may hold values from 0 to 127, all different within a row
- vert_count: int32 [128], P('rep'), parts along dimension 0, may hold values from 1 to 64
- slash: int32 [128, 32], P('rep'), parts along dimension 0, may hold values from 0 to 95, all different within a row
- slash_count: int32 [128], P('rep'), parts along dimension 0, may hold values from 1 to 32
Outputs:
- attended: bfloat16 [4096, 8192], P(('rep', 'seq')), parts along dimension 0
There are 2 independent parts, one for each index of `rep`. A program takes and returns all parts, laid end to end along the dimension named above; each array names one. Nothing has to cross between parts.
Inputs may be any that keep to these rules, and one draw needn't show every extreme that they name: `vertical`: each row holds 64 different key block numbers; head h uses the first vert_count[h] of them. `slash`: each row holds 32 different numbers; head h uses the first slash_count[h] of them, each number s naming the slash offset s + 1 blocks.
All inputs are finite; a program needn't handle non-finite values.
Results may differ from a plain program's by a relative error of at most 0.007.
Values may be sent and summed in bfloat16 or wider, within the bound.
No kernel may reach another device: no remote copies, remote signals or barrier semaphores. Data moves between devices by JAX's collectives and lax.ppermute only.
A program may use at most 128 MiB of HBM per device.

v0:
```python
import math
import jax
import jax.numpy as jnp
from jax import lax
from jax.sharding import PartitionSpec as P

QUERY_HEADS = 64
KV_HEADS = 8
HEAD_DIM = 128
BLOCK = 64
TURN = 4


def swapped(x, axis, bit):
    return lax.ppermute(x, axis, [(i, i ^ 1 << bit) for i in range(lax.axis_size(axis))])


def absorb(state, scores, valid, combine):
    peak, total, summed = state
    scores = jnp.where(valid, scores, -jnp.inf)
    new_peak = jnp.maximum(peak, jnp.max(scores, axis=1))
    factor = jnp.exp(peak - new_peak)
    weights = jnp.exp(scores - new_peak[:, None])
    total = total * factor + jnp.sum(weights, axis=1)
    summed = summed * factor[:, None] + combine(weights.astype(jnp.bfloat16))
    return (new_peak, total, summed)


def attend(
    query_blocks, storage, slot_of, head, first, stride, vertical, vert_count, slash, slash_count
):
    count_rows, block, width = query_blocks.shape
    total_blocks = storage.shape[0] // block
    cache = storage.reshape(total_blocks, block, 2 * width)
    scale = 1.0 / math.sqrt(width)
    rows = count_rows * block
    absolute = (
        total_blocks
        - count_rows * stride
        + first
        + stride * jnp.arange(count_rows, dtype=jnp.int32)
    )
    verticals = vertical[head]
    live_vert = vert_count[head]
    offsets = slash[head] + 1
    live_slash = slash_count[head]
    lanes = jnp.arange(TURN, dtype=jnp.int32)
    marks = jnp.arange(verticals.shape[0], dtype=jnp.int32) < live_vert
    flat_query = query_blocks.reshape(rows, width)
    diagonal = cache[slot_of(absolute)]
    scores = (
        jnp.einsum(
            "rqd,rkd->rqk", query_blocks, diagonal[:, :, :width], preferred_element_type=jnp.float32
        )
        * scale
    )
    causal = jnp.arange(block)[:, None] >= jnp.arange(block)[None, :]
    scores = jnp.where(causal[None], scores, -jnp.inf)
    peak = jnp.max(scores, axis=2)
    weights = jnp.exp(scores - peak[:, :, None])
    total = jnp.sum(weights, axis=2)
    summed = jnp.einsum(
        "rqk,rkd->rqd",
        weights.astype(jnp.bfloat16),
        diagonal[:, :, width:],
        preferred_element_type=jnp.float32,
    )
    state = (peak.reshape(rows), total.reshape(rows), summed.reshape(rows, width))

    def widen(usable):
        return jnp.broadcast_to(usable[:, None, :, None], (count_rows, block, TURN, block)).reshape(
            rows, TURN * block
        )

    def vertical_turn(step, state):
        picked = lax.dynamic_slice_in_dim(verticals, step * TURN, TURN)
        keys_here = cache[slot_of(picked)].reshape(TURN * block, 2 * width)
        scores = (
            lax.dot_general(
                flat_query,
                keys_here[:, :width],
                (((1,), (1,)), ((), ())),
                preferred_element_type=jnp.float32,
            )
            * scale
        )
        usable = (step * TURN + lanes < live_vert)[None, :] & (picked[None, :] < absolute[:, None])

        def combine(rounded):
            return jnp.dot(rounded, keys_here[:, width:], preferred_element_type=jnp.float32)

        return absorb(state, scores, widen(usable), combine)

    state = lax.fori_loop(0, (live_vert + TURN - 1) // TURN, vertical_turn, state)

    def slash_turn(step, state):
        picked = lax.dynamic_slice_in_dim(offsets, step * TURN, TURN)
        target = absolute[:, None] - picked[None, :]
        keys_here = cache[slot_of(target)].reshape(count_rows, TURN * block, 2 * width)
        scores = (
            jnp.einsum(
                "rqd,rkd->rqk",
                query_blocks,
                keys_here[:, :, :width],
                preferred_element_type=jnp.float32,
            ).reshape(rows, TURN * block)
            * scale
        )
        covered = jnp.any(
            (target[:, :, None] == verticals[None, None, :]) & marks[None, None, :], axis=2
        )
        usable = (step * TURN + lanes < live_slash)[None, :] & jnp.logical_not(covered)

        def combine(rounded):
            return jnp.einsum(
                "rqk,rkd->rqd",
                rounded.reshape(count_rows, block, TURN * block),
                keys_here[:, :, width:],
                preferred_element_type=jnp.float32,
            ).reshape(rows, width)

        return absorb(state, scores, widen(usable), combine)

    state = lax.fori_loop(0, (live_slash + TURN - 1) // TURN, slash_turn, state)
    peak, total, summed = state
    return (summed / total[:, None]).astype(jnp.bfloat16).reshape(count_rows, block, width)


def body(queries, keys, values, vertical, vert_count, slash, slash_count):
    seq_count = lax.axis_size("seq")
    position = lax.axis_index("seq")
    query_rows = queries.shape[0]
    key_rows = keys.shape[0]
    group_devices = seq_count // KV_HEADS
    local_cache = jnp.concatenate(
        [keys.reshape(key_rows, KV_HEADS, HEAD_DIM), values.reshape(key_rows, KV_HEADS, HEAD_DIM)],
        axis=2,
    )
    piece_rows = key_rows // group_devices
    pieces = (
        local_cache.reshape(group_devices, piece_rows, KV_HEADS, 2 * HEAD_DIM)
        .transpose(1, 2, 0, 3)
        .reshape(piece_rows, seq_count, 2 * HEAD_DIM)
    )
    stacked = lax.all_to_all(pieces, "seq", split_axis=1, concat_axis=0, tiled=True).reshape(
        1, seq_count * piece_rows, 2 * HEAD_DIM
    )
    for level in range(group_devices.bit_length() - 1):
        partner = swapped(stacked, "seq", level)
        upper_side = position // 2**level % 2 == 1
        lower = jnp.where(upper_side, partner, stacked)
        upper = jnp.where(upper_side, stacked, partner)
        stacked = jnp.concatenate([lower, upper], axis=0)
    storage = stacked.reshape(group_devices * seq_count * piece_rows, 2 * HEAD_DIM)
    device_blocks = key_rows // BLOCK
    piece_blocks = piece_rows // BLOCK

    def slot_of(index):
        sender = index // device_blocks
        within = index % device_blocks
        return (
            within // piece_blocks * (seq_count * piece_blocks)
            + sender * piece_blocks
            + within % piece_blocks
        )

    per_device = QUERY_HEADS // seq_count
    blocks = queries.reshape(query_rows // BLOCK, BLOCK, QUERY_HEADS, HEAD_DIM)
    gathered = lax.all_to_all(blocks, "seq", split_axis=2, concat_axis=0, tiled=True)
    results = []
    for local in range(per_device):
        results.append(
            attend(
                gathered[:, :, local, :],
                storage,
                slot_of,
                position * per_device + local,
                0,
                1,
                vertical,
                vert_count,
                slash,
                slash_count,
            )
        )
    answer = lax.all_to_all(
        jnp.stack(results, axis=2), "seq", split_axis=0, concat_axis=2, tiled=True
    )
    return answer.reshape(query_rows, QUERY_HEADS * HEAD_DIM)


def solution(mesh):
    return jax.shard_map(
        body,
        mesh=mesh,
        in_specs=(
            P(("rep", "seq"), None),
            P(("rep", "seq"), None),
            P(("rep", "seq"), None),
            P("rep", None),
            P("rep"),
            P("rep", None),
            P("rep"),
        ),
        out_specs=P(("rep", "seq"), None),
        check_vma=False,
    )
```

profile of v0, /device:TPU:0, one launch (start us, length us, event | category | flops | bytes accessed | tf_op | source)
XLA Modules:
  0.0 1188.1 jit_solution(315355499021703888)
XLA Ops:
  3.9 8.3 all-to-all-start
  17.1 38.2 %all-to-all-done = bf16[256,16,256]{2,0,1:T(8,128)(2,1)S(1)} async-done(((bf16[256,16,256]{2,0,1:T(8,128)(2,1)}), bf16[256,16,256]{2,0,1:T(8,128)(2,1)S(1)}, u32[]{:S(2)}, u32[]{:S(2)}) %all-to-all-start) | async-done | bytes 2097184 | tf_op jit(solution)/shard_map/all_to_all | solution.py:145
  56.6 10.0 all-to-all-start.1
  76.7 32.6 %all-to-all-done.1 = bf16[2,64,64,128]{3,1,0,2:T(8,128)(2,1)S(1)} async-done(((bf16[2,64,64,128]{3,1,0,2:T(8,128)(2,1)}), bf16[2,64,64,128]{3,1,0,2:T(8,128)(2,1)S(1)}, u32[]{:S(2)}, u32[]{:S(2)}) %all-to-all-start.1) | async-done | bytes 2097184 | tf_op jit(solution)/shard_map/all_to_all | solution.py:169
  112.2 23.4 %collective-permute-done = bf16[1,4096,256]{2,1,0:T(8,128)(2,1)} collective-permute-done((bf16[1,4096,256]{2,1,0:T(8,128)(2,1)}, bf16[1,4096,256]{2,1,0:T(8,128)(2,1)}, u32[]{:S(2)}, u32[]{:S(2)}) %collective-permute-start) | collective-permute-done | bytes 2097184 | tf_op jit(solution)/shard_map/ppermute | solution.py:15
  155.0 12.7 %while.148 = (s32[]{:T(128)}, f32[2048]{0:T(1024)S(1)}, f32[2048]{0:T(1024)S(1)}, f32[2048,128]{1,0:T(8,128)S(1)}, s32[]{:T(128)}, /*index=5*/s32[]{:T(128)}, s3...) while((s32[]{:T(128)}, f32[2048]{0:T(1024)S(1)}, ...), condition=%wide.region_5.6_spmd.clone, body=%wide.region_2.5_spmd.clone.sunk | while | flops 272635360 | bytes 11539231 | solution.py:94
  157.7 4.2 reshape.1859
  167.7 126.9 %while.152 = (s32[]{:T(128)}, f32[2048]{0:T(1024)S(1)}, f32[2048]{0:T(1024)S(1)}, f32[2048,128]{1,0:T(8,128)S(1)}, s32[]{:T(128)}, /*index=5*/s32[]{:T(128)}, s3...) while((s32[]{:T(128)}, f32[2048]{0:T(1024)S(1)}, ...), condition=%wide.region_10.11_spmd.clone.clone, body=%wide.region_6.10_spmd.clone.clone.sunk | while | flops 274762880 | bytes 32220464 | solution.py:124
  170.1 5.0 gather_fusion
  188.2 5.0 gather_fusion
  197.2 4.1 fusion.329
  206.3 5.0 gather_fusion
  224.5 5.0 gather_fusion
  233.4 4.1 fusion.329
  242.6 5.0 gather_fusion
  251.6 4.1 fusion.329
  260.7 5.0 gather_fusion
  269.7 4.1 fusion.329
  278.8 5.0 gather_fusion
  295.7 195.0 %while.149 = (s32[]{:T(128)}, f32[2048]{0:T(1024)S(1)}, f32[2048]{0:T(1024)S(1)}, f32[2048,128]{1,0:T(8,128)S(1)}, s32[]{:T(128)}, /*index=5*/s32[]{:T(128)}, s3...) while((s32[]{:T(128)}, f32[2048]{0:T(1024)S(1)}, ...), condition=%wide.region_16.17_spmd.clone, body=%wide.region_13.16_spmd.clone.sunk | while | flops 272635360 | bytes 11539231 | solution.py:94
  297.8 4.2 reshape.1862
  310.0 4.2 reshape.1862
  322.2 4.2 reshape.1862
  334.4 4.2 reshape.1862
  346.6 4.2 reshape.1862
  358.8 4.2 reshape.1862
  371.0 4.2 reshape.1862
  383.1 4.2 reshape.1862
  395.3 4.2 reshape.1862
  407.5 4.2 reshape.1862
  419.7 4.2 reshape.1862
  431.9 4.2 reshape.1862
  444.1 4.2 reshape.1862
  456.3 4.2 reshape.1862
  468.5 4.2 reshape.1862
  480.7 4.2 reshape.1862
  490.7 125.9 %while.153 = (s32[]{:T(128)}, f32[2048]{0:T(1024)S(1)}, f32[2048]{0:T(1024)S(1)}, f32[2048,128]{1,0:T(8,128)S(1)}, s32[]{:T(128)}, /*index=5*/s32[]{:T(128)}, s3...) while((s32[]{:T(128)}, f32[2048]{0:T(1024)S(1)}, ...), condition=%wide.region_21.22_spmd.clone.clone, body=%wide.region_17.21_spmd.clone.clone.sunk | while | flops 274762880 | bytes 34317640 | solution.py:124
  493.1 5.0 gather_fusion.1
  508.8 5.0 gather_fusion.1
  524.6 5.0 gather_fusion.1
  540.3 5.0 gather_fusion.1
  556.0 5.0 gather_fusion.1
  571.7 5.0 gather_fusion.1
  587.4 5.0 gather_fusion.1
  603.1 5.0 gather_fusion.1
  616.7 81.9 %while.150 = (s32[]{:T(128)}, f32[2048]{0:T(1024)S(1)}, f32[2048]{0:T(1024)S(1)}, f32[2048,128]{1,0:T(8,128)S(1)}, s32[]{:T(128)}, /*index=5*/s32[]{:T(128)}, s3...) while((s32[]{:T(128)}, f32[2048]{0:T(1024)S(1)}, ...), condition=%wide.region_27.28_spmd.clone, body=%wide.region_24.27_spmd.clone.sunk | while | flops 272635360 | bytes 11539231 | solution.py:94
  698.7 126.0 %while.154 = (s32[]{:T(128)}, f32[2048]{0:T(1024)S(1)}, f32[2048]{0:T(1024)S(1)}, f32[2048,128]{1,0:T(8,128)S(1)}, s32[]{:T(128)}, /*index=5*/s32[]{:T(128)}, s3...) while((s32[]{:T(128)}, f32[2048]{0:T(1024)S(1)}, ...), condition=%wide.region_32.33_spmd.clone.clone, body=%wide.region_28.32_spmd.clone.clone.sunk | while | flops 274762880 | bytes 32220464 | solution.py:124
  701.1 5.0 gather_fusion.2
  719.1 5.0 gather_fusion.2
  737.1 5.0 gather_fusion.2
  755.0 5.0 gather_fusion.2
  773.0 5.0 gather_fusion.2
  791.0 5.0 gather_fusion.2
  809.0 5.0 gather_fusion.2
  824.8 61.2 %while.151 = (s32[]{:T(128)}, f32[2048]{0:T(1024)S(1)}, f32[2048]{0:T(1024)S(1)}, f32[2048,128]{1,0:T(8,128)S(1)}, s32[]{:T(128)}, /*index=5*/s32[]{:T(128)}, s3...) while((s32[]{:T(128)}, f32[2048]{0:T(1024)S(1)}, ...), condition=%wide.region_38.39_spmd.clone, body=%wide.region_35.38_spmd.clone.sunk | while | flops 272635360 | bytes 11539231 | solution.py:94
  827.2 4.2 reshape.1868
  839.4 4.2 reshape.1868
  851.6 4.2 reshape.1868
  863.8 4.2 reshape.1868
  876.0 4.2 reshape.1868
  886.0 35.8 %while.155 = (s32[]{:T(128)}, f32[2048]{0:T(1024)S(1)}, f32[2048]{0:T(1024)S(1)}, f32[2048,128]{1,0:T(8,128)S(1)}, s32[]{:T(128)}, /*index=5*/s32[]{:T(128)}, s3...) while((s32[]{:T(128)}, f32[2048]{0:T(1024)S(1)}, ...), condition=%wide.region_43.44_spmd.clone.clone, body=%wide.region_39.43_spmd.clone.clone.sunk | while | flops 274762880 | bytes 32220464 | solution.py:124
  888.3 5.0 gather_fusion.3
  906.2 5.0 gather_fusion.3
  924.7 258.7 %all_to_all.48 = bf16[32,64,4,128]{3,1,2,0:T(8,128)(2,1)S(1)} all-to-all(bf16[32,64,4,128]{3,1,2,0:T(8,128)(2,1)S(1)} %pad_maximum_fusion.1), channel_id=1, replica_groups=mesh['rep'=2,'seq'=16] {'seq'}, dimensions={0} | all-to-all | bytes 4194304 | tf_op jit(solution)/shard_map/all_to_all | solution.py:186
  (1089 shorter events, 576.9 us)
Async XLA Ops:
  0.0 1.6 copy-start.14
  3.9 51.4 %all-to-all-start = ((bf16[256,16,256]{2,0,1:T(8,128)(2,1)}), bf16[256,16,256]{2,0,1:T(8,128)(2,1)S(1)}, u32[]{:S(2)}, u32[]{:S(2)}) async-start(bf16[256,16,256]{2,0,1:T(8,128)(2,1)} %bitcast.1), calls=%async_computation | async-start | bytes 4194304 | tf_op jit(solution)/shard_map/all_to_all | solution.py:145
  17.1 51.5 %copy-start.19 = (s32[64]{0:T(128)S(1)}, s32[64]{0:T(128)}, u32[]{:S(2)}) copy-start(s32[64]{0:T(128)} %param.29) | copy-start | bytes 772
  17.1 51.5 %copy-start.20 = (s32[64]{0:T(128)S(1)}, s32[64]{0:T(128)}, u32[]{:S(2)}) copy-start(s32[64]{0:T(128)} %param.27) | copy-start | bytes 772
  17.1 57.3 %copy-start.16 = (s32[64,32]{0,1:T(8,128)S(1)}, s32[64,32]{0,1:T(8,128)}, u32[]{:S(2)}) copy-start(s32[64,32]{0,1:T(8,128)} %param.28) | copy-start | bytes 24580
  55.3 1.4 copy-start.9
  56.6 52.6 %all-to-all-start.1 = ((bf16[2,64,64,128]{3,1,0,2:T(8,128)(2,1)}), bf16[2,64,64,128]{3,1,0,2:T(8,128)(2,1)S(1)}, u32[]{:S(2)}, u32[]{:S(2)}) async-start(bf16[2,64,64,128]{3,1,0,2:T(8,128)(2,1)} %copy.39), calls=%async_computation.1 | async-start | bytes 4194304 | tf_op jit(solution)/shard_map/all_to_all | solution.py:169
  66.7 69.0 %collective-permute-start = (bf16[1,4096,256]{2,1,0:T(8,128)(2,1)}, bf16[1,4096,256]{2,1,0:T(8,128)(2,1)}, u32[]{:S(2)}, u32[]{:S(2)}) collective-permute-start(bf16[1,4096,256]{2,1,0:T(8,128)(2,1)} %bitcast.307), channel_id=1, source_target_pairs={{0,1},{1,0},{2,3},{3,2},{4,5},{5,4},{6,7},{7,6},{8,9},{9,8},{10,11... | collective-permute-start | bytes 6291464 | tf_op jit(solution)/shard_map/ppermute | solution.py:15
  109.4 2.8 copy-start.8
  109.5 26.2 %copy-start.10 = (bf16[256,16,256]{2,0,1:T(8,128)(2,1)S(1)}, bf16[256,16,256]{2,0,1:T(8,128)(2,1)}, u32[]{:S(2)}) copy-start(bf16[256,16,256]{2,0,1:T(8,128)(2,1)} %copy-done.9) | copy-start | bytes 6291460
  142.7 4.6 copy-start.6
  150.4 1.7 copy-start.7
  179.1 4.1 copy-start.2
  197.2 4.1 copy-start.2
  215.3 4.1 copy-start.2
  233.4 4.1 copy-start.2
  251.6 4.1 copy-start.2
  269.7 4.1 copy-start.2
  287.8 4.1 copy-start.2
  294.6 1.1 copy-start.1
  294.6 1.1 copy-start.12
  493.1 5.0 copy-start.15
  502.1 3.0 copy-start.3
  508.8 5.0 copy-start.15
  517.8 3.0 copy-start.3
  524.6 5.0 copy-start.15
  533.5 3.0 copy-start.3
  540.3 5.0 copy-start.15
  549.2 3.0 copy-start.3
  556.0 5.0 copy-start.15
  564.9 3.0 copy-start.3
  571.7 5.0 copy-start.15
  580.7 3.0 copy-start.3
  587.4 5.0 copy-start.15
  596.4 3.0 copy-start.3
  603.1 5.0 copy-start.15
  612.1 3.0 copy-start.3
  698.6 126.0 %copy-start.17 = (f32[32,64]{1,0:T(8,128)S(1)}, f32[32,64]{1,0:T(8,128)}, u32[]{:S(2)}) copy-start(f32[32,64]{1,0:T(8,128)} %fusion.203) | copy-start | bytes 24580
  698.6 126.1 %copy-start = (f32[32,64,128]{2,1,0:T(8,128)S(1)}, f32[32,64,128]{2,1,0:T(8,128)}, u32[]{:S(2)}) copy-start(f32[32,64,128]{2,1,0:T(8,128)} %fusion.204) | copy-start | bytes 3145732
  698.7 126.1 %copy-start.11 = (f32[2048]{0:T(1024)S(1)}, f32[2048]{0:T(1024)}, u32[]{:S(2)}) copy-start(f32[2048]{0:T(1024)} %reshape.1697) | copy-start | bytes 24580
  698.7 126.1 %copy-start.18 = (s32[1,64]{1,0:T(1,128)S(1)}, s32[1,64]{1,0:T(1,128)}, u32[]{:S(2)}) copy-start(s32[1,64]{1,0:T(1,128)} %get-tuple-element.2841) | copy-start | bytes 772
  710.1 4.0 copy-start.4
  728.0 4.0 copy-start.4
  746.0 4.0 copy-start.4
  764.0 4.0 copy-start.4
  782.0 4.0 copy-start.4
  800.0 4.0 copy-start.4
  818.0 4.0 copy-start.4
  824.8 61.2 %copy-start.21 = (s32[32]{0:T(128)S(1)}, s32[32]{0:T(128)}, u32[]{:S(2)}) copy-start(s32[32]{0:T(128)} %get-tuple-element.2840) | copy-start | bytes 388
  886.0 35.8 %copy-start.13 = (f32[2048]{0:T(1024)S(1)}, f32[2048]{0:T(1024)}, u32[]{:S(2)}) copy-start(f32[2048]{0:T(1024)} %copy-done.12) | copy-start | bytes 24580
  897.2 4.0 copy-start.5
  915.1 4.0 copy-start.5
where the time goes:
time: 1200 us; the launch traced here: 1190 us
  local copies, waits for them, and re-layouts  393 us (33%)
  matrix products  271 us (23%)
  blocking collectives  259 us (22%)
  other arithmetic  139 us (12%)
  waiting for transfers between devices  94.2 us (8%)
  starting transfers between devices  20.3 us (2%)
    all_to_all x1, blocking collectives, body(): lax.all_to_all(jnp.stack(results, axis=2), 'seq', split_axis=0, concat_ax...  259 us
    gather x24, local copies, waits for them, and re-layouts, slash_turn(): cache[slot_of(target)].reshape(count_rows, TURN * block, 2 * width)  120 us
    reshape x30, local copies, waits for them, and re-layouts, widen(): jnp.broadcast_to(usable[:, None, :, None], (count_rows, block, TURN, block))  118 us
    dot_general x24, matrix products, slash_turn(): jnp.einsum('rqd,rkd->rqk', query_blocks, keys_here[:, :, :width], preferr...  91.6 us
    dot_general x24, matrix products, combine(): jnp.einsum('rqk,rkd->rqd', rounded.reshape(count_rows, block, TURN * bloc...  88.2 us
    gather x30, local copies, waits for them, and re-layouts, vertical_turn(): keys_here = cache[slot_of(picked)].reshape(TURN * block, 2 * width)  82.2 us
    dot_general x30, matrix products, vertical_turn(): lax.dot_general(flat_query, keys_here[:, :width], (((1,), (1,)), ((), ())...  51.4 us
    all_to_all x1, waiting for transfers between devices, body(): lax.all_to_all(pieces, 'seq', split_axis=1, concat_axis=0, tiled=True)  38.2 us
  transfers between devices with their start and end apart: 3, of which 3 were waited for; matrix products, arithmetic and copies ran while one was open for 1% of the time, Pallas kernels for 0%

commit v1 on v0

--- a/solution.py
+++ b/solution.py
@@ -1,3 +1,4 @@
+import functools
 import math
 import jax
 import jax.numpy as jnp
@@ -9,6 +10,40 @@
 HEAD_DIM = 128
 BLOCK = 64
 TURN = 4
+
+
+def knots_move(chunk, along_dim, block_in):
+    before = chunk.shape
+    outer = chunk.reshape(
+        *before[:along_dim], block_in, before[along_dim] // block_in, *before[along_dim + 1 :]
+    )
+    return jnp.moveaxis(outer, along_dim, 0)
+
+
+def sheet_do(original, axis_no):
+    original = jnp.moveaxis(original, 0, axis_no)
+    later = original.shape
+    return original.reshape(
+        *later[:axis_no], later[axis_no] * later[axis_no + 1], *later[axis_no + 2 :]
+    )
+
+
+def watch_core(content, mesh_dim, x0, matrix):
+    tmp, mat_out = (lax.axis_size(mesh_dim), lax.axis_index(mesh_dim))
+    ready = knots_move(content, x0, tmp)
+    b_now = ready
+    for dev_i in range(1, tmp):
+        front, known = ((mat_out + dev_i) % tmp, (mat_out - dev_i) % tmp)
+        moved = lax.dynamic_index_in_dim(ready, front, 0)
+        so_far_all = []
+        for it in range(tmp):
+            so_far_all.append((it, (it + dev_i) % tmp))
+        local_out = lax.ppermute(moved, mesh_dim, so_far_all)
+        b_now = lax.dynamic_update_slice_in_dim(b_now, local_out, known, axis=0)
+    return sheet_do(b_now, matrix)
+
+
+attach_stops_all = functools.partial(watch_core, mesh_dim="seq", x0=0, matrix=2)
 
 
 def swapped(x, axis, bit):
@@ -183,9 +218,7 @@
                 slash_count,
             )
         )
-    answer = lax.all_to_all(
-        jnp.stack(results, axis=2), "seq", split_axis=0, concat_axis=2, tiled=True
-    )
+    answer = attach_stops_all(jnp.stack(results, axis=2))
     return answer.reshape(query_rows, QUERY_HEADS * HEAD_DIM)
 
 

time: 1200 us -> 1100 us (0.917)
  blocking collectives: 259 us -> 0 us
  starting transfers between devices: 20.3 us -> 236 us
  local copies, waits for them, and re-layouts: 393 us -> 356 us
  matrix products: 271 us -> 237 us
    all_to_all x1 -> x0, blocking collectives: 259 us -> none  [body(): lax.all_to_all(jnp.stack(results, axis=2), 'seq', split_axis=0, concat_ax...]
    ppermute x0 -> x15, starting transfers between devices: none -> 216 us  [watch_core(): local_out = lax.ppermute(moved, mesh_dim, so_far_all)]
    reshape x30, local copies, waits for them, and re-layouts: 118 us -> 88.7 us  [widen(): jnp.broadcast_to(usable[:, None, :, None], (count_rows, block, TURN, block))]
    broadcast_in_dim x78, local copies, waits for them, and re-layouts: 36.3 us -> 15.9 us  [widen(): jnp.broadcast_to(usable[:, None, :, None], (count_rows, block, TURN, block))]
    dot_general x30, matrix products: 51.4 us -> 35.7 us  [vertical_turn(): lax.dot_general(flat_query, keys_here[:, :width], (((1,), (1,)), ((), ())...]
    ppermute x0 -> x15, waiting for transfers between devices: none -> 12.7 us  [watch_core(): local_out = lax.ppermute(moved, mesh_dim, so_far_all)]
  transfers between devices with their start and end apart: 3 -> 18, of which waited for: 3 -> 7; matrix products, arithmetic and copies ran while one was open for 1% -> 1% of each run, Pallas kernels for 0% -> 0%
where the time goes in v1:
time: 1100 us; the launch traced here: 1090 us
  local copies, waits for them, and re-layouts  356 us (32%)
  matrix products  237 us (22%)
  starting transfers between devices  236 us (21%)
  other arithmetic  140 us (13%)
  waiting for transfers between devices  104 us (9%)
    ppermute x15, starting transfers between devices, watch_core(): local_out = lax.ppermute(moved, mesh_dim, so_far_all)  216 us
    gather x24, local copies, waits for them, and re-layouts, slash_turn(): cache[slot_of(target)].reshape(count_rows, TURN * block, 2 * width)  120 us
    reshape x30, local copies, waits for them, and re-layouts, widen(): jnp.broadcast_to(usable[:, None, :, None], (count_rows, block, TURN, block))  88.7 us
    dot_general x24, matrix products, slash_turn(): jnp.einsum('rqd,rkd->rqk', query_blocks, keys_here[:, :, :width], preferr...  82.7 us
    gather x30, local copies, waits for them, and re-layouts, vertical_turn(): keys_here = cache[slot_of(picked)].reshape(TURN * block, 2 * width)  82.2 us
    dot_general x24, matrix products, combine(): jnp.einsum('rqk,rkd->rqd', rounded.reshape(count_rows, block, TURN * bloc...  80 us
    all_to_all x1, waiting for transfers between devices, body(): lax.all_to_all(pieces, 'seq', split_axis=1, concat_axis=0, tiled=True)  38.2 us
    dot_general x30, matrix products, vertical_turn(): lax.dot_general(flat_query, keys_here[:, :width], (((1,), (1,)), ((), ())...  35.7 us
  transfers between devices with their start and end apart: 18, of which 7 were waited for; matrix products, arithmetic and copies ran while one was open for 1% of the time, Pallas kernels for 0%

profile of v1, /device:TPU:0, one launch (start us, length us, event | category | flops | bytes accessed | tf_op | source)
XLA Modules:
  0.0 1086.3 jit_solution(1096041139637235611)
XLA Ops:
  3.9 8.3 all-to-all-start
  17.1 38.2 %all-to-all-done = bf16[256,16,256]{2,0,1:T(8,128)(2,1)S(1)} async-done(((bf16[256,16,256]{2,0,1:T(8,128)(2,1)}), bf16[256,16,256]{2,0,1:T(8,128)(2,1)S(1)}, u32[]{:S(2)}, u32[]{:S(2)}) %all-to-all-start) | async-done | bytes 2097184 | tf_op jit(solution)/shard_map/all_to_all | solution.py:180
  56.6 10.0 all-to-all-start.1
  76.7 32.6 %all-to-all-done.1 = bf16[2,64,64,128]{3,1,0,2:T(8,128)(2,1)S(1)} async-done(((bf16[2,64,64,128]{3,1,0,2:T(8,128)(2,1)}), bf16[2,64,64,128]{3,1,0,2:T(8,128)(2,1)S(1)}, u32[]{:S(2)}, u32[]{:S(2)}) %all-to-all-start.1) | async-done | bytes 2097184 | tf_op jit(solution)/shard_map/all_to_all | solution.py:204
  115.1 20.6 %collective-permute-done = bf16[1,4096,256]{2,1,0:T(8,128)(2,1)} collective-permute-done((bf16[1,4096,256]{2,1,0:T(8,128)(2,1)}, bf16[1,4096,256]{2,1,0:T(8,128)(2,1)}, u32[]{:S(2)}, u32[]{:S(2)}) %collective-permute-start) | collective-permute-done | bytes 2097184 | tf_op jit(solution)/shard_map/ppermute | solution.py:50
  153.7 12.4 %while.148 = (s32[]{:T(128)}, f32[2048]{0:T(1024)S(1)}, f32[2048]{0:T(1024)S(1)}, f32[2048,128]{1,0:T(8,128)S(1)}, s32[]{:T(128)}, /*index=5*/s32[]{:T(128)}, s3...) while((s32[]{:T(128)}, f32[2048]{0:T(1024)S(1)}, ...), condition=%wide.region_5.6_spmd.clone, body=%wide.region_2.5_spmd.clone.sunk | while | flops 272635360 | bytes 11539231 | solution.py:129
  156.1 4.2 reshape.1863
  166.1 126.2 %while.152 = (s32[]{:T(128)}, f32[2048]{0:T(1024)S(1)}, f32[2048]{0:T(1024)S(1)}, f32[2048,128]{1,0:T(8,128)S(1)}, s32[]{:T(128)}, /*index=5*/s32[]{:T(128)}, s3...) while((s32[]{:T(128)}, f32[2048]{0:T(1024)S(1)}, ...), condition=%wide.region_10.11_spmd.clone.clone, body=%wide.region_6.10_spmd.clone.clone.sunk | while | flops 274762880 | bytes 32220464 | solution.py:159
  168.5 5.0 gather_fusion
  173.5 3.8 bitcast_reduce_fusion.8
  177.5 4.0 fusion.329
  186.5 5.0 gather_fusion
  191.5 3.8 bitcast_reduce_fusion.8
  195.5 4.0 fusion.329
  204.5 5.0 gather_fusion
  209.5 3.8 bitcast_reduce_fusion.8
  213.5 4.0 fusion.329
  222.6 5.0 gather_fusion
  227.5 3.8 bitcast_reduce_fusion.8
  231.5 4.0 fusion.329
  240.6 5.0 gather_fusion
  245.6 3.8 bitcast_reduce_fusion.8
  249.6 4.0 fusion.329
  258.6 5.0 gather_fusion
  263.6 3.8 bitcast_reduce_fusion.8
  267.6 4.0 fusion.329
  276.7 5.0 gather_fusion
  281.6 3.8 bitcast_reduce_fusion.8
  285.6 4.0 fusion.329
  294.6 163.6 %while.149 = (s32[]{:T(128)}, f32[2048]{0:T(1024)S(1)}, f32[2048]{0:T(1024)S(1)}, f32[2048,128]{1,0:T(8,128)S(1)}, s32[]{:T(128)}, /*index=5*/s32[]{:T(128)}, s3...) while((s32[]{:T(128)}, f32[2048]{0:T(1024)S(1)}, ...), condition=%wide.region_16.17_spmd.clone, body=%wide.region_13.16_spmd.clone.sunk | while | flops 272635360 | bytes 11539231 | solution.py:129
  458.1 125.9 %while.153 = (s32[]{:T(128)}, f32[2048]{0:T(1024)S(1)}, f32[2048]{0:T(1024)S(1)}, f32[2048,128]{1,0:T(8,128)S(1)}, s32[]{:T(128)}, /*index=5*/s32[]{:T(128)}, s3...) while((s32[]{:T(128)}, f32[2048]{0:T(1024)S(1)}, ...), condition=%wide.region_21.22_spmd.clone.clone, body=%wide.region_17.21_spmd.clone.clone.sunk | while | flops 274762880 | bytes 34317640 | solution.py:159
  460.6 5.0 gather_fusion.1
  476.3 5.0 gather_fusion.1
  492.0 5.0 gather_fusion.1
  497.1 3.8 bitcast_reduce_fusion.9
  507.7 5.0 gather_fusion.1
  512.8 3.8 bitcast_reduce_fusion.9
  523.5 5.0 gather_fusion.1
  528.5 3.8 bitcast_reduce_fusion.9
  539.2 5.0 gather_fusion.1
  554.9 5.0 gather_fusion.1
  570.6 5.0 gather_fusion.1
  586.3 67.3 %while.150 = (s32[]{:T(128)}, f32[2048]{0:T(1024)S(1)}, f32[2048]{0:T(1024)S(1)}, f32[2048,128]{1,0:T(8,128)S(1)}, s32[]{:T(128)}, /*index=5*/s32[]{:T(128)}, s3...) while((s32[]{:T(128)}, f32[2048]{0:T(1024)S(1)}, ...), condition=%wide.region_27.28_spmd.clone, body=%wide.region_24.27_spmd.clone.sunk | while | flops 272635360 | bytes 11539231 | solution.py:129
  653.6 111.4 %while.154 = (s32[]{:T(128)}, f32[2048]{0:T(1024)S(1)}, f32[2048]{0:T(1024)S(1)}, f32[2048,128]{1,0:T(8,128)S(1)}, s32[]{:T(128)}, /*index=5*/s32[]{:T(128)}, s3...) while((s32[]{:T(128)}, f32[2048]{0:T(1024)S(1)}, ...), condition=%wide.region_32.33_spmd.clone.clone, body=%wide.region_28.32_spmd.clone.clone.sunk | while | flops 274762880 | bytes 23831828 | solution.py:159
  655.9 5.0 gather_fusion.2
  671.8 5.0 gather_fusion.2
  687.8 5.0 gather_fusion.2
  703.7 5.0 gather_fusion.2
  719.6 5.0 gather_fusion.2
  735.5 5.0 gather_fusion.2
  751.4 5.0 gather_fusion.2
  767.3 42.5 %while.151 = (s32[]{:T(128)}, f32[2048]{0:T(1024)S(1)}, f32[2048]{0:T(1024)S(1)}, f32[2048,128]{1,0:T(8,128)S(1)}, s32[]{:T(128)}, /*index=5*/s32[]{:T(128)}, s3...) while((s32[]{:T(128)}, f32[2048]{0:T(1024)S(1)}, ...), condition=%wide.region_38.39_spmd.clone, body=%wide.region_35.38_spmd.clone.sunk | while | flops 272635360 | bytes 11539231 | solution.py:129
  809.8 31.4 %while.155 = (s32[]{:T(128)}, f32[2048]{0:T(1024)S(1)}, f32[2048]{0:T(1024)S(1)}, f32[2048,128]{1,0:T(8,128)S(1)}, s32[]{:T(128)}, /*index=5*/s32[]{:T(128)}, s3...) while((s32[]{:T(128)}, f32[2048]{0:T(1024)S(1)}, ...), condition=%wide.region_43.44_spmd.clone.clone, body=%wide.region_39.43_spmd.clone.clone.sunk | while | flops 274762880 | bytes 34317640 | solution.py:159
  812.0 5.0 gather_fusion.3
  827.7 5.0 gather_fusion.3
  843.1 4.9 pad_maximum_fusion.1
  848.3 8.4 collective-permute-done.1
  859.6 9.5 collective-permute-start.2
  869.1 160.6 %collective-permute-start.3 = (bf16[1,2,64,4,128]{4,3,0,2,1:T(4,128)(2,1)}, bf16[1,2,64,4,128]{4,3,0,2,1:T(4,128)(2,1)}, u32[]{:S(2)}, u32[]{:S(2)}) collective-permute-start(bf16[1,2,64,4,128]{4,3,0,2,1:T(4,128)(2,1)} %get-tuple-element.2199), channel_id=1, source_target_pairs={{0,3},{1,4},{2,5},{3,6},{4,7},{5,8},{6,9},{7,10},{8,11},{9,12},{10... | collective-permute-start | bytes 393224 | tf_op jit(solution)/shard_map/ppermute | solution.py:41
  1029.7 11.8 %collective-permute-start.4 = (bf16[1,2,64,4,128]{4,3,0,2,1:T(4,128)(2,1)}, bf16[1,2,64,4,128]{4,3,0,2,1:T(4,128)(2,1)S(1)}, u32[]{:S(2)}, u32[]{:S(2)}) collective-permute-start(bf16[1,2,64,4,128]{4,3,0,2,1:T(4,128)(2,1)} %get-tuple-element.2198), channel_id=1, source_target_pairs={{0,4},{1,5},{2,6},{3,7},{4,8},{5,9},{6,10},{7,11},{8,12},{9,13},{1... | collective-permute-start | bytes 393224 | tf_op jit(solution)/shard_map/ppermute | solution.py:41
  1041.9 6.7 collective-permute-start.7
  1051.4 3.9 collective-permute-start.9
  1055.4 9.5 collective-permute-start.10
  1073.9 4.1 collective-permute-start.14
  (1133 shorter events, 554.8 us)
Async XLA Ops:
  0.0 1.6 copy-start.16
  3.9 51.4 %all-to-all-start = ((bf16[256,16,256]{2,0,1:T(8,128)(2,1)}), bf16[256,16,256]{2,0,1:T(8,128)(2,1)S(1)}, u32[]{:S(2)}, u32[]{:S(2)}) async-start(bf16[256,16,256]{2,0,1:T(8,128)(2,1)} %bitcast.1), calls=%async_computation | async-start | bytes 4194304 | tf_op jit(solution)/shard_map/all_to_all | solution.py:180
  17.1 51.5 %copy-start.22 = (s32[64]{0:T(128)S(1)}, s32[64]{0:T(128)}, u32[]{:S(2)}) copy-start(s32[64]{0:T(128)} %param.29) | copy-start | bytes 772
  17.1 51.5 %copy-start.23 = (s32[64]{0:T(128)S(1)}, s32[64]{0:T(128)}, u32[]{:S(2)}) copy-start(s32[64]{0:T(128)} %param.27) | copy-start | bytes 772
  17.1 57.3 %copy-start.19 = (s32[64,32]{0,1:T(8,128)S(1)}, s32[64,32]{0,1:T(8,128)}, u32[]{:S(2)}) copy-start(s32[64,32]{0,1:T(8,128)} %param.28) | copy-start | bytes 24580
  55.3 1.4 copy-start.10
  56.6 52.6 %all-to-all-start.1 = ((bf16[2,64,64,128]{3,1,0,2:T(8,128)(2,1)}), bf16[2,64,64,128]{3,1,0,2:T(8,128)(2,1)S(1)}, u32[]{:S(2)}, u32[]{:S(2)}) async-start(bf16[2,64,64,128]{3,1,0,2:T(8,128)(2,1)} %copy.53), calls=%async_computation.1 | async-start | bytes 4194304 | tf_op jit(solution)/shard_map/all_to_all | solution.py:204
  66.7 69.0 %collective-permute-start = (bf16[1,4096,256]{2,1,0:T(8,128)(2,1)}, bf16[1,4096,256]{2,1,0:T(8,128)(2,1)}, u32[]{:S(2)}, u32[]{:S(2)}) collective-permute-start(bf16[1,4096,256]{2,1,0:T(8,128)(2,1)} %bitcast.305), channel_id=1, source_target_pairs={{0,1},{1,0},{2,3},{3,2},{4,5},{5,4},{6,7},{7,6},{8,9},{9,8},{10,11... | collective-permute-start | bytes 6291464 | tf_op jit(solution)/shard_map/ppermute | solution.py:50
  109.3 1.3 copy-start.9
  112.4 30.3 %copy-start.8 = (bf16[16,2,64,4,128]{4,2,1,0,3:T(8,128)(2,1)}, bf16[16,2,64,4,128]{4,2,1,0,3:T(8,128)(2,1)S(1)}, u32[]{:S(2)}) copy-start(bf16[16,2,64,4,128]{4,2,1,0,3:T(8,128)(2,1)S(1)} %copy.55) | copy-start | bytes 6291460
  112.4 23.3 %copy-start.11 = (bf16[256,16,256]{2,0,1:T(8,128)(2,1)S(1)}, bf16[256,16,256]{2,0,1:T(8,128)(2,1)}, u32[]{:S(2)}) copy-start(bf16[256,16,256]{2,0,1:T(8,128)(2,1)} %copy-done.10) | copy-start | bytes 6291460
  142.7 3.2 copy-start.6
  149.0 1.7 copy-start.7
  177.5 4.0 copy-start.1
  195.5 4.0 copy-start.1
  213.5 4.0 copy-start.1
  231.5 4.0 copy-start.1
  249.6 4.0 copy-start.1
  267.6 4.0 copy-start.1
  285.6 4.0 copy-start.1
  460.6 5.0 copy-start.18
  469.6 3.0 copy-start.2
  476.3 5.0 copy-start.18
  485.3 3.0 copy-start.2
  492.0 5.0 copy-start.18
  501.0 3.0 copy-start.2
  507.7 5.0 copy-start.18
  516.7 3.0 copy-start.2
  523.4 5.0 copy-start.18
  532.4 3.0 copy-start.2
  539.2 5.0 copy-start.18
  548.1 3.0 copy-start.2
  554.9 5.0 copy-start.18
  563.8 3.0 copy-start.2
  570.6 5.0 copy-start.18
  579.5 3.0 copy-start.2
  584.1 2.2 copy-start.5
  765.0 2.2 copy-start.20
  765.0 2.2 copy-start
  765.1 2.2 copy-start.4
  765.1 2.2 copy-start.15
  765.1 2.2 copy-start.21
  767.3 42.5 %copy-start.24 = (s32[32]{0:T(128)S(1)}, s32[32]{0:T(128)}, u32[]{:S(2)}) copy-start(s32[32]{0:T(128)} %get-tuple-element.2855) | copy-start | bytes 388
  812.0 5.0 copy-start.17
  821.0 3.0 copy-start.3
  827.7 5.0 copy-start.17
  836.7 3.0 copy-start.3
  841.2 1.5 copy-start.13
  841.2 1.8 copy-start.14
  848.1 8.7 collective-permute-start.1
  859.6 182.3 %collective-permute-start.2 = (bf16[1,2,64,4,128]{4,3,0,2,1:T(4,128)(2,1)}, bf16[1,2,64,4,128]{4,3,0,2,1:T(4,128)(2,1)}, u32[]{:S(2)}, u32[]{:S(2)}) collective-permute-start(bf16[1,2,64,4,128]{4,3,0,2,1:T(4,128)(2,1)} %get-tuple-element.2200), channel_id=1, source_target_pairs={{0,2},{1,3},{2,4},{3,5},{4,6},{5,7},{6,8},{7,9},{8,10},{9,11},{10,... | collective-permute-start | bytes 393224 | tf_op jit(solution)/shard_map/ppermute | solution.py:41
  869.1 180.4 %collective-permute-start.3 = (bf16[1,2,64,4,128]{4,3,0,2,1:T(4,128)(2,1)}, bf16[1,2,64,4,128]{4,3,0,2,1:T(4,128)(2,1)}, u32[]{:S(2)}, u32[]{:S(2)}) collective-permute-start(bf16[1,2,64,4,128]{4,3,0,2,1:T(4,128)(2,1)} %get-tuple-element.2199), channel_id=1, source_target_pairs={{0,3},{1,4},{2,5},{3,6},{4,7},{5,8},{6,9},{7,10},{8,11},{9,12},{10... | collective-permute-start | bytes 393224 | tf_op jit(solution)/shard_map/ppermute | solution.py:41
  1029.7 21.8 %collective-permute-start.4 = (bf16[1,2,64,4,128]{4,3,0,2,1:T(4,128)(2,1)}, bf16[1,2,64,4,128]{4,3,0,2,1:T(4,128)(2,1)S(1)}, u32[]{:S(2)}, u32[]{:S(2)}) collective-permute-start(bf16[1,2,64,4,128]{4,3,0,2,1:T(4,128)(2,1)} %get-tuple-element.2198), channel_id=1, source_target_pairs={{0,4},{1,5},{2,6},{3,7},{4,8},{5,9},{6,10},{7,11},{8,12},{9,13},{1... | collective-permute-start | bytes 393224 | tf_op jit(solution)/shard_map/ppermute | solution.py:41
  1041.4 14.0 %collective-permute-start.5 = (bf16[1,2,64,4,128]{4,3,0,2,1:T(4,128)(2,1)S(1)}, bf16[1,2,64,4,128]{4,3,0,2,1:T(4,128)(2,1)S(1)}, u32[]{:S(2)}, u32[]{:S(2)}) collective-permute-start(bf16[1,2,64,4,128]{4,3,0,2,1:T(4,128)(2,1)S(1)} %get-tuple-element.2197), channel_id=1, source_target_pairs={{0,5},{1,6},{2,7},{3,8},{4,9},{5,10},{6,11},{7,12},{8,13},{9,14},{... | collective-permute-start | bytes 393224 | tf_op jit(solution)/shard_map/ppermute | solution.py:41
  1041.9 23.2 %collective-permute-start.6 = (bf16[1,2,64,4,128]{4,3,0,2,1:T(4,128)(2,1)S(1)}, bf16[1,2,64,4,128]{4,3,0,2,1:T(4,128)(2,1)S(1)}, u32[]{:S(2)}, u32[]{:S(2)}) collective-permute-start(bf16[1,2,64,4,128]{4,3,0,2,1:T(4,128)(2,1)S(1)} %get-tuple-element.2196), channel_id=1, source_target_pairs={{0,6},{1,7},{2,8},{3,9},{4,10},{5,11},{6,12},{7,13},{8,14},{9,15},... | collective-permute-start | bytes 393224 | tf_op jit(solution)/shard_map/ppermute | solution.py:41
  1041.9 26.4 %collective-permute-start.7 = (bf16[1,2,64,4,128]{4,3,0,2,1:T(4,128)(2,1)S(1)}, bf16[1,2,64,4,128]{4,3,0,2,1:T(4,128)(2,1)S(1)}, u32[]{:S(2)}, u32[]{:S(2)}) collective-permute-start(bf16[1,2,64,4,128]{4,3,0,2,1:T(4,128)(2,1)S(1)} %get-tuple-element.2195), channel_id=1, source_target_pairs={{0,7},{1,8},{2,9},{3,10},{4,11},{5,12},{6,13},{7,14},{8,15},{9,0},... | collective-permute-start | bytes 393224 | tf_op jit(solution)/shard_map/ppermute | solution.py:41
  1049.5 22.3 %collective-permute-start.8 = (bf16[1,2,64,4,128]{4,3,0,2,1:T(4,128)(2,1)S(1)}, bf16[1,2,64,4,128]{4,3,0,2,1:T(4,128)(2,1)S(1)}, u32[]{:S(2)}, u32[]{:S(2)}) collective-permute-start(bf16[1,2,64,4,128]{4,3,0,2,1:T(4,128)(2,1)S(1)} %get-tuple-element.2194), channel_id=1, source_target_pairs={{0,8},{1,9},{2,10},{3,11},{4,12},{5,13},{6,14},{7,15},{8,0},{9,1},... | collective-permute-start | bytes 393224 | tf_op jit(solution)/shard_map/ppermute | solution.py:41
  1051.4 22.5 %collective-permute-start.9 = (bf16[1,2,64,4,128]{4,3,0,2,1:T(4,128)(2,1)S(1)}, bf16[1,2,64,4,128]{4,3,0,2,1:T(4,128)(2,1)S(1)}, u32[]{:S(2)}, u32[]{:S(2)}) collective-permute-start(bf16[1,2,64,4,128]{4,3,0,2,1:T(4,128)(2,1)S(1)} %get-tuple-element.2193), channel_id=1, source_target_pairs={{0,9},{1,10},{2,11},{3,12},{4,13},{5,14},{6,15},{7,0},{8,1},{9,2},... | collective-permute-start | bytes 393224 | tf_op jit(solution)/shard_map/ppermute | solution.py:41
  1055.4 22.7 %collective-permute-start.10 = (bf16[1,2,64,4,128]{4,3,0,2,1:T(4,128)(2,1)S(1)}, bf16[1,2,64,4,128]{4,3,0,2,1:T(4,128)(2,1)S(1)}, u32[]{:S(2)}, u32[]{:S(2)}) collective-permute-start(bf16[1,2,64,4,128]{4,3,0,2,1:T(4,128)(2,1)S(1)} %get-tuple-element.2192), channel_id=1, source_target_pairs={{0,10},{1,11},{2,12},{3,13},{4,14},{5,15},{6,0},{7,1},{8,2},{9,3},... | collective-permute-start | bytes 393224 | tf_op jit(solution)/shard_map/ppermute | solution.py:41
  1065.1 13.4 %collective-permute-start.11 = (bf16[1,2,64,4,128]{4,3,0,2,1:T(4,128)(2,1)S(1)}, bf16[1,2,64,4,128]{4,3,0,2,1:T(4,128)(2,1)S(1)}, u32[]{:S(2)}, u32[]{:S(2)}) collective-permute-start(bf16[1,2,64,4,128]{4,3,0,2,1:T(4,128)(2,1)S(1)} %get-tuple-element.2191), channel_id=1, source_target_pairs={{0,11},{1,12},{2,13},{3,14},{4,15},{5,0},{6,1},{7,2},{8,3},{9,4},{... | collective-permute-start | bytes 393224 | tf_op jit(solution)/shard_map/ppermute | solution.py:41
  1068.3 10.6 collective-permute-start.12
  1071.8 7.2 collective-permute-start.13
  1073.9 6.7 collective-permute-start.14
  1078.2 5.0 collective-permute-start.15
  (1 other events, 1.2 us)
